TPU v7x, 768 devices: a whole 4x8x12 slice. The times are simulated.
768 devices in a mesh: grp: 24 (over x, z_hi, core), bn: 32 (over z_lo, y).
Axes of the slice: x: 4, y: 8, z: 12 (z_hi: 3, z_lo: 4; z = z_hi * 4 + z_lo), core: 2. Of those that a mesh axis runs over, the one named last changes fastest.
Arguments:
- images: bfloat16 [96, 128, 64, 1024], P('grp', 'bn'), parts along dimension 0, may hold values from -64 to 64
- w_reduce: bfloat16 [1024, 256], replicated, may hold values from -0.1875 to 0.1875
- w_spatial: bfloat16 [3, 3, 256, 256], replicated, may hold values from -0.125 to 0.125
- w_expand: bfloat16 [256, 1024], replicated, may hold values from -0.375 to 0.375
- gain_first: float32 [256], replicated, may hold values from 0.25 to 1.75
- shift_first: float32 [256], replicated, may hold values from -3 to 3
- gain_middle: float32 [256], replicated, may hold values from 0.25 to 1.75
- shift_middle: float32 [256], replicated, may hold values from -3 to 3
- gain_last: float32 [1024], replicated, may hold values from 0.25 to 1.75
- shift_last: float32 [1024], replicated, may hold values from -3 to 3
Outputs:
- block_out: bfloat16 [96, 128, 64, 1024], P('grp', 'bn'), parts along dimension 0
There are 24 independent parts, one for each index of `grp`. A program takes and returns all parts, laid end to end along the dimension named above; an argument that names none is the same for every part. Nothing has to cross between parts.
All inputs are finite; a program needn't handle non-finite values.
Results may differ from a plain program's by a relative error of at most 0.0034.
Values may be sent and summed in bfloat16 or wider, within the bound.
No kernel may reach another device: no remote copies, remote signals or barrier semaphores. Data moves between devices by JAX's collectives and lax.ppermute only.
A program may use at most 32 MiB of HBM per device.

v0:
```python
import jax
import jax.numpy as jnp
from jax import lax
from jax.sharding import PartitionSpec as P

epsilon = 1e-05


def copy_for_each(value, axis):
    copies = jnp.broadcast_to(value, (lax.axis_size(axis), *value.shape))
    return lax.all_to_all(copies, axis, split_axis=0, concat_axis=0, tiled=True)


def joined_along(blocks, dim):
    blocks = jnp.moveaxis(blocks, 0, dim)
    dims = blocks.shape
    return blocks.reshape(*dims[:dim], dims[dim] * dims[dim + 1], *dims[dim + 2 :])


def gather_directly(value, axis, dim):
    blocks = copy_for_each(value, axis)
    return joined_along(blocks, dim)


def padded_2(cells, sides, width):
    for axis, dim in sides:
        count = lax.axis_size(axis)
        ends = count - 1
        head = lax.slice_in_dim(cells, 0, width, axis=dim)
        tail = lax.slice_in_dim(cells, cells.shape[dim] - width, cells.shape[dim], axis=dim)
        cells = jnp.concatenate(
            [
                lax.ppermute(tail, axis, [(i, (i + 1) % count) for i in range(ends)]),
                cells,
                lax.ppermute(head, axis, [((i + 1) % count, i) for i in range(ends)]),
            ],
            axis=dim,
        )
    return cells


def group_sum(partial_value):
    gathered = gather_directly(partial_value[None], "bn", 0)
    return jnp.sum(gathered, axis=0)


def statistics(values, population):
    pooled_axes = (0, 1, 2)
    moments = group_sum(
        jnp.stack([jnp.sum(values, axis=pooled_axes), jnp.sum(values * values, axis=pooled_axes)])
    )
    average = moments[0] / population
    spread = moments[1] / population - average * average
    return (average, spread)


def apply_norm(values, average, spread, gain, shift):
    return (values - average) * (gain * lax.rsqrt(spread + epsilon)) + shift


def normalize(values, gain, shift, population):
    average, spread = statistics(values, population)
    return apply_norm(values, average, spread, gain, shift)


def body(
    images,
    w_reduce,
    w_spatial,
    w_expand,
    gain_first,
    shift_first,
    gain_middle,
    shift_middle,
    gain_last,
    shift_last,
):
    population = images.shape[0] * images.shape[1] * images.shape[2] * lax.axis_size("bn")
    first = jnp.einsum("nhwc,cd->nhwd", images, w_reduce, preferred_element_type=jnp.float32)
    hidden_first = jax.nn.relu(normalize(first, gain_first, shift_first, population)).astype(
        jnp.bfloat16
    )
    padded = padded_2(hidden_first, (("bn", 1),), 1)
    middle = lax.conv_general_dilated(
        padded,
        w_spatial,
        (1, 1),
        ((0, 0), (1, 1)),
        dimension_numbers=("NHWC", "HWIO", "NHWC"),
        preferred_element_type=jnp.float32,
    )
    hidden_middle = jax.nn.relu(normalize(middle, gain_middle, shift_middle, population)).astype(
        jnp.bfloat16
    )
    last = jnp.einsum("nhwc,cd->nhwd", hidden_middle, w_expand, preferred_element_type=jnp.float32)
    summed = normalize(last, gain_last, shift_last, population) + images.astype(jnp.float32)
    return jax.nn.relu(summed).astype(jnp.bfloat16)


def solution(mesh):
    placed = (P("grp", "bn", None, None), P(), P(), P(), P(), P(), P(), P(), P(), P())
    return jax.shard_map(
        body, mesh=mesh, in_specs=placed, out_specs=P("grp", "bn", None, None), check_vma=False
    )
```

profile of v0, /device:TPU:4, one launch (start us, length us, event | category | flops | bytes accessed | tf_op | source)
XLA Modules:
  0.0 78.4 jit_solution(12715058689153848425)
XLA Ops:
  0.0 0.0 copy-start
  0.0 0.0 copy-start.6
  0.0 0.0 copy-start.8
  0.0 2.5 %fusion.9 = (f32[256]{0:T(256)S(1)}, f32[256]{0:T(256)S(1)}, f32[4,4,64,256]{3,2,1,0:T(8,128)S(1)}) fusion(bf16[4,4,64,1024]{3,2,1,0:T(8,128)(2,1)} %param.10, bf16[1024,256]{1,0:T(8,128)(2,1)} %param.11), kind=kOutput, calls=%fused_computation.32 | convolution fusion | flops 537656832 | bytes 3672064 | tf_op jit(solution)/shard_map/nhwc,cd->nhwd/dot_general | solution.py:79
  2.6 23.0 %all_to_all.15 = f32[32,1,2,256]{3,2,1,0:T(2,128)S(1)} all-to-all(f32[32,1,2,256]{3,2,1,0:T(2,128)S(1)} %broadcast_in_dim.6), channel_id=1, replica_groups=mesh['grp'=24,'bn'=32] {'bn'}, dimensions={0} | all-to-all | bytes 131072 | tf_op jit(solution)/shard_map/all_to_all | solution.py:11
  25.6 0.0 copy-done.6
  25.6 0.0 copy-done.8
  25.7 0.2 maximum_convert_fusion.2
  25.9 2.7 %collective-permute-start = (bf16[4,1,64,256]{3,2,1,0:T(8,128)(2,1)S(1)}, bf16[4,1,64,256]{3,2,1,0:T(8,128)(2,1)S(1)}, u32[]{:S(2)}, u32[]{:S(2)}) collective-permute-start(bf16[4,1,64,256]{3,2,1,0:T(8,128)(2,1)S(1)} %get-tuple-element.11), channel_id=1, source_target_pairs={{0,1},{1,2},{2,3},{3,4},{4,5},{5,6},{6,7},{7,8},{8,9},{9,10},{10,1... | collective-permute-start | bytes 393224 | tf_op jit(solution)/shard_map/ppermute | solution.py:33
  28.5 1.3 %collective-permute-start.1 = (bf16[4,1,64,256]{3,2,1,0:T(8,128)(2,1)S(1)}, bf16[4,1,64,256]{3,2,1,0:T(8,128)(2,1)S(1)}, u32[]{:S(2)}, u32[]{:S(2)}) collective-permute-start(bf16[4,1,64,256]{3,2,1,0:T(8,128)(2,1)S(1)} %get-tuple-element.12), channel_id=1, source_target_pairs={{1,0},{2,1},{3,2},{4,3},{5,4},{6,5},{7,6},{8,7},{9,8},{10,9},{11,1... | collective-permute-start | bytes 393224 | tf_op jit(solution)/shard_map/ppermute | solution.py:35
  29.8 1.2 %collective-permute-done = bf16[4,1,64,256]{3,2,1,0:T(8,128)(2,1)S(1)} collective-permute-done((bf16[4,1,64,256]{3,2,1,0:T(8,128)(2,1)S(1)}, bf16[4,1,64,256]{3,2,1,0:T(8,128)(2,1)S(1)}, u32[]{:S(2)}, u32[]{:S(2)}) %collective-permute-start) | collective-permute-done | bytes 131104 | tf_op jit(solution)/shard_map/ppermute | solution.py:33
  31.0 4.4 %collective-permute-done.1 = bf16[4,1,64,256]{3,2,1,0:T(8,128)(2,1)S(1)} collective-permute-done((bf16[4,1,64,256]{3,2,1,0:T(8,128)(2,1)S(1)}, bf16[4,1,64,256]{3,2,1,0:T(8,128)(2,1)S(1)}, u32[]{:S(2)}, u32[]{:S(2)}) %collective-permute-start.1) | collective-permute-done | bytes 131104 | tf_op jit(solution)/shard_map/ppermute | solution.py:35
  35.4 0.1 maximum_bitcast_fusion
  35.5 0.6 copy.39
  36.1 0.3 pad.clone
  36.5 0.0 copy-start.9
  36.5 0.1 slice.38
  36.5 0.5 fusion.1
  37.0 0.0 copy-done
  37.0 0.1 copy-done.9
  37.1 0.0 copy-start.7
  37.1 0.0 copy-start.5
  37.2 1.6 %select_reduce_fusion.1 = (f32[256]{0:T(256)S(1)}, f32[256]{0:T(256)S(1)}, f32[4,32,9,256]{3,1,2,0:T(8,128)S(1)}) fusion(pred[32,9]{0,1:T(8,128)(4,1)S(1)} %copy-done.9, bf16[3,3,256,256]{3,2,1,0:T(8,128)(2,1)S(1)} %copy-done, bf16[6,4,8,11,256]{4,1,3,2,0:T(4,128)(2,1)S(1)} %fusion.1), kind=kOutput, calls=%fused_computation.7 | convolution fusion | flops 1360723456 | bytes 3442976 | tf_op jit(solution)/shard_map/conv_general_dilated | solution.py:84
  38.8 16.7 %all_to_all.16 = f32[32,1,2,256]{3,2,1,0:T(2,128)S(1)} all-to-all(f32[32,1,2,256]{3,2,1,0:T(2,128)S(1)} %broadcast_in_dim.7), channel_id=1, replica_groups=mesh['grp'=24,'bn'=32] {'bn'}, dimensions={0} | all-to-all | bytes 131072 | tf_op jit(solution)/shard_map/all_to_all | solution.py:11
  55.5 0.0 copy-done.7
  55.5 0.0 copy-done.5
  55.5 0.2 maximum_convert_fusion.1
  55.7 0.0 copy-start.2
  55.8 0.5 copy.24
  56.2 0.2 slice.41
  56.4 0.4 copy-done.2
  56.8 0.0 copy-start.4
  56.8 0.0 copy-start.1
  56.8 0.0 copy-start.3
  56.8 2.6 %fusion.8 = (f32[1024]{0:T(1024)S(1)}, f32[1024]{0:T(1024)S(1)}, f32[4,4,64,1024]{3,2,1,0:T(8,128)}) fusion(bf16[256,1024]{1,0:T(8,128)(2,1)S(1)} %copy-done.2, bf16[4,4,64,256]{3,0,2,1:T(4,128)(2,1)S(1)} %slice.41), kind=kOutput, calls=%fused_computation.31 | convolution fusion | flops 540014592 | bytes 5251072 | tf_op jit(solution)/shard_map/nhwc,cd->nhwd/dot_general | solution.py:95
  59.5 0.1 broadcast_in_dim.8
  59.5 14.2 %all_to_all.17 = f32[32,1,2,1024]{3,2,1,0:T(2,128)S(1)} all-to-all(f32[32,1,2,1024]{3,2,1,0:T(2,128)S(1)} %broadcast_in_dim.8), channel_id=1, replica_groups=mesh['grp'=24,'bn'=32] {'bn'}, dimensions={0} | all-to-all | bytes 524288 | tf_op jit(solution)/shard_map/all_to_all | solution.py:11
  73.7 0.1 reduce_sum.89
  73.8 0.0 copy-done.4
  73.9 0.0 copy-done.1
  73.9 0.0 copy-done.3
  73.9 4.5 %maximum_convert_fusion = bf16[4,4,64,1024]{3,2,1,0:T(8,128)(2,1)} fusion(bf16[4,4,64,1024]{3,2,1,0:T(8,128)(2,1)S(1)} %copy-done.1, f32[4,4,64,1024]{3,2,1,0:T(8,128)} %get-tuple-element.21, f32[1024]{0:T(1024)S(1)} %copy-done.3, f32[1024]{0:T(1024)S(1)} %rsqrt_multiply_fusion, f32[1024]{0:T(1024)S(1)} %bitcast.46), kind=kLoop, calls=%fused_computation | loop fusion | flops 7340032 | bytes 8400896 | tf_op jit(solution)/shard_map/convert_element_type | solution.py:97
  (14 shorter events, 0.2 us)
Async XLA Ops:
  0.0 37.0 %copy-start = (bf16[3,3,256,256]{3,2,1,0:T(8,128)(2,1)S(1)}, bf16[3,3,256,256]{3,2,1,0:T(8,128)(2,1)}, u32[]{:S(2)}) copy-start(bf16[3,3,256,256]{3,2,1,0:T(8,128)(2,1)} %param.12) | copy-start | bytes 3538948
  0.0 25.6 %copy-start.6 = (f32[256]{0:T(256)S(1)}, f32[256]{0:T(256)}, u32[]{:S(2)}) copy-start(f32[256]{0:T(256)} %param.14) | copy-start | bytes 3076
  0.0 25.6 %copy-start.8 = (f32[256]{0:T(256)S(1)}, f32[256]{0:T(256)}, u32[]{:S(2)}) copy-start(f32[256]{0:T(256)} %param.15) | copy-start | bytes 3076
  25.9 5.2 %collective-permute-start = (bf16[4,1,64,256]{3,2,1,0:T(8,128)(2,1)S(1)}, bf16[4,1,64,256]{3,2,1,0:T(8,128)(2,1)S(1)}, u32[]{:S(2)}, u32[]{:S(2)}) collective-permute-start(bf16[4,1,64,256]{3,2,1,0:T(8,128)(2,1)S(1)} %get-tuple-element.11), channel_id=1, source_target_pairs={{0,1},{1,2},{2,3},{3,4},{4,5},{5,6},{6,7},{7,8},{8,9},{9,10},{10,1... | collective-permute-start | bytes 393224 | tf_op jit(solution)/shard_map/ppermute | solution.py:33
  28.5 6.9 %collective-permute-start.1 = (bf16[4,1,64,256]{3,2,1,0:T(8,128)(2,1)S(1)}, bf16[4,1,64,256]{3,2,1,0:T(8,128)(2,1)S(1)}, u32[]{:S(2)}, u32[]{:S(2)}) collective-permute-start(bf16[4,1,64,256]{3,2,1,0:T(8,128)(2,1)S(1)} %get-tuple-element.12), channel_id=1, source_target_pairs={{1,0},{2,1},{3,2},{4,3},{5,4},{6,5},{7,6},{8,7},{9,8},{10,9},{11,1... | collective-permute-start | bytes 393224 | tf_op jit(solution)/shard_map/ppermute | solution.py:35
  36.5 0.7 copy-start.9
  37.1 18.4 %copy-start.7 = (f32[256]{0:T(256)S(1)}, f32[256]{0:T(256)}, u32[]{:S(2)}) copy-start(f32[256]{0:T(256)} %param.16) | copy-start | bytes 3076
  37.1 18.4 %copy-start.5 = (f32[256]{0:T(256)S(1)}, f32[256]{0:T(256)}, u32[]{:S(2)}) copy-start(f32[256]{0:T(256)} %param.17) | copy-start | bytes 3076
  55.7 1.0 %copy-start.2 = (bf16[256,1024]{1,0:T(8,128)(2,1)S(1)}, bf16[256,1024]{1,0:T(8,128)(2,1)}, u32[]{:S(2)}) copy-start(bf16[256,1024]{1,0:T(8,128)(2,1)} %param.13) | copy-start | bytes 1572868
  56.8 17.1 %copy-start.4 = (f32[1024]{0:T(1024)S(1)}, f32[1024]{0:T(1024)}, u32[]{:S(2)}) copy-start(f32[1024]{0:T(1024)} %param.18) | copy-start | bytes 12292
  56.8 17.1 %copy-start.1 = (bf16[4,4,64,1024]{3,2,1,0:T(8,128)(2,1)S(1)}, bf16[4,4,64,1024]{3,2,1,0:T(8,128)(2,1)}, u32[]{:S(2)}) copy-start(bf16[4,4,64,1024]{3,2,1,0:T(8,128)(2,1)} %param.10) | copy-start | bytes 6291460
  56.8 17.1 %copy-start.3 = (f32[1024]{0:T(1024)S(1)}, f32[1024]{0:T(1024)}, u32[]{:S(2)}) copy-start(f32[1024]{0:T(1024)} %param.19) | copy-start | bytes 12292
where the time goes:
time: 78.7 us; the launch traced here: 78.4 us
  blocking collectives  53.9 us (68%)
  matrix products  6.72 us (9%)
  other arithmetic  5.65 us (7%)
  waiting for transfers between devices  5.56 us (7%)
  starting transfers between devices  3.98 us (5%)
  local copies, waits for them, and re-layouts  2.31 us (3%)
    all_to_all x3, blocking collectives, copy_for_each(): return lax.all_to_all(copies, axis, split_axis=0, concat_axis=0, tiled=True)  53.9 us
    convert_element_type x1, other arithmetic, body(): return jax.nn.relu(summed).astype(jnp.bfloat16)  4.47 us
    ppermute x1, waiting for transfers between devices, padded_2(): lax.ppermute(head, axis, [((i + 1) % count, i) for i in range(ends)])  4.36 us
    ppermute x1, starting transfers between devices, padded_2(): lax.ppermute(tail, axis, [(i, (i + 1) % count) for i in range(ends)])  2.68 us
    dot_general x1, matrix products, body(): jnp.einsum('nhwc,cd->nhwd', hidden_middle, w_expand, preferred_element_ty...  2.65 us
    dot_general x1, matrix products, body(): jnp.einsum('nhwc,cd->nhwd', images, w_reduce, preferred_element_type=jnp....  2.49 us
    conv_general_dilated x1, matrix products, body(): lax.conv_general_dilated(padded, w_spatial, (1, 1), ((0, 0), (1, 1)), dim...  1.58 us
  transfers between devices with their start and end apart: 2, of which 2 were waited for; matrix products, arithmetic and copies ran while one was open for 0% of the time, Pallas kernels for 0%

commit v1 on v0

v1 whole, which is shorter than its diff:
```python
import jax
import jax.numpy as jnp
from jax import lax
from jax.experimental import pallas as pl
from jax.experimental.pallas import tpu as pltpu
from jax.sharding import PartitionSpec as P

epsilon = 1e-05
f32 = jnp.float32
bf16 = jnp.bfloat16

VM = pl.BlockSpec(memory_space=pltpu.VMEM)
SM = pl.BlockSpec(memory_space=pltpu.SMEM)
HB = pl.BlockSpec(memory_space=pltpu.HBM)


def in_vmem(value):
    return pltpu.with_memory_space_constraint(value, pltpu.VMEM)


def in_hbm(value):
    return pltpu.with_memory_space_constraint(value, pltpu.HBM)


def call(kernel, outs, in_specs, out_specs, scratch=(), flops=0):
    return pl.pallas_call(
        kernel,
        out_shape=outs,
        in_specs=in_specs,
        out_specs=out_specs,
        scratch_shapes=list(scratch),
        compiler_params=pltpu.CompilerParams(vmem_limit_bytes=16 << 20),
        cost_estimate=pl.CostEstimate(flops=flops, bytes_accessed=1 << 20, transcendentals=0),
    )


def eights(block):
    return jnp.sum(block.reshape(block.shape[0] // 8, 8, block.shape[1]), axis=0)


def store_sums(out, total, squares):
    out[0:1, :] = jnp.sum(total, axis=0, keepdims=True)
    out[1:2, :] = jnp.sum(squares, axis=0, keepdims=True)


def factors(gathered, gain, shift, population):
    sums = jnp.sum(gathered[...], axis=0)
    average = sums[0:1, :] / population
    spread = sums[1:2, :] / population - average * average
    return average, gain[...] * lax.rsqrt(spread + epsilon), shift[...]


def reduce_kernel(place, images, weight, first, near, far, sums, kept, w_vmem, sem):
    imgs, rows, wid, ch = images.shape
    copies = [pltpu.make_async_copy(weight, w_vmem, sem.at[imgs])]
    copies += [pltpu.make_async_copy(images.at[n], kept.at[n], sem.at[n]) for n in range(imgs)]
    for c in copies:
        c.start()
    for c in copies:
        c.wait()
    even = place[0] % 2 == 0
    total = squares = None
    for n in range(imgs):
        x = kept[n].reshape(rows * wid, ch)
        y = jnp.dot(x, w_vmem[...], preferred_element_type=f32)
        for r in range(rows):
            first[r, n * wid : (n + 1) * wid, :] = y[r * wid : (r + 1) * wid]
        head, tail = y[:wid].astype(bf16), y[(rows - 1) * wid :].astype(bf16)
        near[n * wid : (n + 1) * wid, :] = jnp.where(even, tail, head)
        far[n * wid : (n + 1) * wid, :] = jnp.where(even, head, tail)
        a, b = eights(y), eights(y * y)
        total, squares = (a, b) if n == 0 else (total + a, squares + b)
    store_sums(sums, total, squares)


def spread_columns(hidden, out, wid):
    count, c = hidden.shape
    column = lax.broadcasted_iota(jnp.int32, (count, 1), 0) % wid
    left = jnp.where(column == 0, 0.0, pltpu.roll(hidden, 1, 0))
    right = jnp.where(column == wid - 1, 0.0, pltpu.roll(hidden, count - 1, 0))
    out[:, 0:c] = left.astype(bf16)
    out[:, c : 2 * c] = hidden.astype(bf16)
    out[:, 2 * c : 3 * c] = right.astype(bf16)


def inner_kernel(wid, population, first, gathered, gain, shift, weight, mid, sums, norm, cells):
    rows = first.shape[0]
    average, factor, bias = factors(gathered, gain, shift, population)
    norm[0:1, :] = average
    norm[1:2, :] = factor
    norm[2:3, :] = bias
    for r in range(rows):
        hidden = jnp.maximum((first[r] - average) * factor + bias, 0.0)
        spread_columns(hidden, cells.at[r], wid)
    k = cells.shape[2]
    total = squares = None
    for r in range(rows):
        lo, hi = max(r - 1, 0), min(r + 2, rows)
        lhs = jnp.concatenate([cells[i] for i in range(lo, hi)], axis=1)
        y = jnp.dot(lhs, weight[(lo - r + 1) * k : (hi - r + 1) * k, :], preferred_element_type=f32)
        mid[r] = y
        if r > 0 and r < rows - 1:
            a, b = eights(y), eights(y * y)
            total, squares = (a, b) if total is None else (total + a, squares + b)
    sums[0] = total
    sums[1] = squares


def edge_kernel(wid, ends, place, mid, near, far, norm, weight, inner, edge, sums, cells):
    rows = mid.shape[0]
    k = cells.shape[2]
    even = place[0] % 2 == 0
    for i in range(2):
        halo = jnp.where(even == (i == 0), far[...], near[...]).astype(f32)
        hidden = jnp.maximum((halo - norm[0:1, :]) * norm[1:2, :] + norm[2:3, :], 0.0)
        hidden = jnp.where(place[0] == (0 if i == 0 else ends), 0.0, hidden)
        spread_columns(hidden, cells.at[i], wid)
    total, squares = inner[0], inner[1]
    for i in range(2):
        y = mid[(rows - 1) * i] + jnp.dot(
            cells[i], weight[2 * i * k : (2 * i + 1) * k, :], preferred_element_type=f32
        )
        edge[i] = y
        total, squares = total + eights(y), squares + eights(y * y)
    store_sums(sums, total, squares)


def expand_kernel(population, mid, edge, gathered, gain, shift, weight, last, sums):
    rows = mid.shape[0]
    average, factor, bias = factors(gathered, gain, shift, population)
    total = squares = None
    for r in range(rows):
        value = edge[0] if r == 0 else edge[1] if r == rows - 1 else mid[r]
        hidden = jnp.maximum((value - average) * factor + bias, 0.0).astype(bf16)
        y = jnp.dot(hidden, weight[...], preferred_element_type=f32)
        last[r] = y
        a, b = eights(y), eights(y * y)
        total, squares = (a, b) if r == 0 else (total + a, squares + b)
    store_sums(sums, total, squares)


def final_kernel(population, last, images, gathered, gain, shift, out, staged, sem):
    imgs, rows, wid, _ = images.shape
    average, factor, bias = factors(gathered, gain, shift, population)
    copies = []
    for n in range(imgs):
        for r in range(rows):
            value = (last[r, n * wid : (n + 1) * wid, :] - average) * factor + bias
            value = value + images[n, r].astype(f32)
            staged[n, r] = jnp.maximum(value, 0.0).astype(bf16)
            copies.append(pltpu.make_async_copy(staged.at[n, r], out.at[n, r], sem.at[n, r]))
            copies[-1].start()
    for c in copies:
        c.wait()


def pairs(start, count):
    firsts = range(start, count - 1, 2)
    return [(i, i + 1) for i in firsts] + [(i + 1, i) for i in firsts]


def to_all(sums, count):
    copies = jnp.broadcast_to(sums, (count, 1, *sums.shape))
    got = lax.all_to_all(copies, "bn", split_axis=0, concat_axis=0, tiled=True)
    return in_vmem(got.reshape(count, *sums.shape))


def body(
    images,
    w_reduce,
    w_spatial,
    w_expand,
    gain_first,
    shift_first,
    gain_middle,
    shift_middle,
    gain_last,
    shift_last,
):
    count = lax.axis_size("bn")
    imgs, rows, wid, ch = images.shape
    mid_ch = w_reduce.shape[1]
    cells = imgs * wid
    population = float(cells * rows * count)
    row = lambda v: in_vmem(v.reshape(1, -1))

    place = lax.axis_index("bn").astype(jnp.int32).reshape(1)
    first, near, far, sums = call(
        reduce_kernel,
        [
            pltpu.VMEM((rows, cells, mid_ch), f32),
            pltpu.VMEM((cells, mid_ch), bf16),
            pltpu.VMEM((cells, mid_ch), bf16),
            pltpu.VMEM((2, mid_ch), f32),
        ],
        [SM, HB, HB],
        [VM] * 4,
        [pltpu.VMEM(images.shape, bf16), pltpu.VMEM(w_reduce.shape, bf16), pltpu.SemaphoreType.DMA((imgs + 1,))],
        2 * cells * rows * ch * mid_ch,
    )(place, in_hbm(images), in_hbm(w_reduce))
    far = lax.ppermute(far, "bn", pairs(1, count))
    near = lax.ppermute(near, "bn", pairs(0, count))

    w_spatial, sums = lax.optimization_barrier((w_spatial, sums))
    gathered = to_all(sums, count)
    weight = in_vmem(w_spatial.reshape(-1, mid_ch))
    middle, inner, norm = call(
        lambda *refs: inner_kernel(wid, population, *refs),
        [
            pltpu.VMEM((rows, cells, mid_ch), f32),
            pltpu.VMEM((2, 8, mid_ch), f32),
            pltpu.VMEM((3, mid_ch), f32),
        ],
        [VM] * 5,
        [VM] * 3,
        [pltpu.VMEM((rows, cells, 3 * mid_ch), bf16)],
        2 * cells * rows * 9 * mid_ch * mid_ch,
    )(first, gathered, row(gain_first), row(shift_first), weight)
    edge, sums = call(
        lambda *refs: edge_kernel(wid, count - 1, *refs),
        [pltpu.VMEM((2, cells, mid_ch), f32), pltpu.VMEM((2, mid_ch), f32)],
        [SM] + [VM] * 6,
        [VM] * 2,
        [pltpu.VMEM((2, cells, 3 * mid_ch), bf16)],
        2 * cells * 6 * mid_ch * mid_ch,
    )(place, middle, in_vmem(near), in_vmem(far), norm, weight, inner)
    images, w_expand, sums = lax.optimization_barrier((images, w_expand, sums))
    gathered = to_all(sums, count)

    last, sums = call(
        lambda *refs: expand_kernel(population, *refs),
        [pltpu.VMEM((rows, cells, ch), f32), pltpu.VMEM((2, ch), f32)],
        [VM] * 6,
        [VM] * 2,
        (),
        2 * cells * rows * ch * mid_ch,
    )(middle, edge, gathered, row(gain_middle), row(shift_middle), in_vmem(w_expand))
    gathered = to_all(sums, count)

    return call(
        lambda *refs: final_kernel(population, *refs),
        jax.ShapeDtypeStruct(images.shape, bf16),
        [VM] * 5,
        HB,
        [pltpu.VMEM(images.shape, bf16), pltpu.SemaphoreType.DMA((imgs, rows))],
        8 * cells * rows * ch,
    )(last, in_vmem(images), gathered, row(gain_last), row(shift_last))


def solution(mesh):
    placed = (P("grp", "bn", None, None), P(), P(), P(), P(), P(), P(), P(), P(), P())
    return jax.shard_map(
        body, mesh=mesh, in_specs=placed, out_specs=P("grp", "bn", None, None), check_vma=False
    )
```

time: 78.7 us -> 64.9 us (0.82)
  blocking collectives: 53.9 us -> 33.5 us
  starting transfers between devices: 3.98 us -> 17.3 us
  Pallas kernels: 0 us -> 6.99 us
  matrix products: 6.72 us -> 0 us
  other arithmetic: 5.65 us -> 0 us
  local copies, waits for them, and re-layouts: 2.31 us -> 0.78 us
    all_to_all x3 -> x2, blocking collectives: 53.9 us -> 33.5 us  [to_all(): got = lax.all_to_all(copies, 'bn', split_axis=0, concat_axis=0, tiled=True)]
    all_to_all x0 -> x1, starting transfers between devices: none -> 12.9 us  [to_all(): got = lax.all_to_all(copies, 'bn', split_axis=0, concat_axis=0, tiled=True)]
    pallas_call x0 -> x5, Pallas kernels: none -> 6.99 us  [the longest x1 2.55 us: body(): call(reduce_kernel, [pltpu.VMEM((rows, cells, mid_ch), f32), pltpu.VMEM((...]
    all_to_all x0 -> x1, waiting for transfers between devices: none -> 5.92 us  [to_all(): got = lax.all_to_all(copies, 'bn', split_axis=0, concat_axis=0, tiled=True)]
    ppermute x2, waiting for transfers between devices: 5.56 us -> 0.01 us  [the longest x1 0.01 us: body(): near = lax.ppermute(near, 'bn', pairs(0, count))]
    dot_general x2 -> x0, matrix products: 5.14 us -> none  [the longest x1 2.65 us: body(): jnp.einsum('nhwc,cd->nhwd', hidden_middle, w_expand, preferred_element_ty...]
    convert_element_type x3 -> x0, other arithmetic: 4.83 us -> none  [the longest x1 4.47 us: body(): return jax.nn.relu(summed).astype(jnp.bfloat16)]
    conv_general_dilated x1 -> x0, matrix products: 1.58 us -> none  [body(): lax.conv_general_dilated(padded, w_spatial, (1, 1), ((0, 0), (1, 1)), dim...]
  transfers between devices with their start and end apart: 2 -> 3, of which waited for: 2 -> 1; matrix products, arithmetic and copies ran while one was open for 0% -> 0% of each run, Pallas kernels for 0% -> 2%
where the time goes in v1:
time: 64.9 us; the launch traced here: 64.7 us
  blocking collectives  33.5 us (52%)
  starting transfers between devices  17.3 us (27%)
  Pallas kernels  6.99 us (11%)
  waiting for transfers between devices  5.93 us (9%)
  local copies, waits for them, and re-layouts  0.78 us (1%)
    all_to_all x2, blocking collectives, to_all(): got = lax.all_to_all(copies, 'bn', split_axis=0, concat_axis=0, tiled=True)  33.5 us
    all_to_all x1, starting transfers between devices, to_all(): got = lax.all_to_all(copies, 'bn', split_axis=0, concat_axis=0, tiled=True)  12.9 us
    all_to_all x1, waiting for transfers between devices, to_all(): got = lax.all_to_all(copies, 'bn', split_axis=0, concat_axis=0, tiled=True)  5.92 us
    ppermute x1, starting transfers between devices, body(): near = lax.ppermute(near, 'bn', pairs(0, count))  3.7 us
    pallas_call x1, Pallas kernels, body(): call(reduce_kernel, [pltpu.VMEM((rows, cells, mid_ch), f32), pltpu.VMEM((...  2.55 us
    pallas_call x1, Pallas kernels, body(): call(lambda *refs: final_kernel(population, *refs), jax.ShapeDtypeStruct(...  1.84 us
  transfers between devices with their start and end apart: 3, of which 1 were waited for; matrix products, arithmetic and copies ran while one was open for 0% of the time, Pallas kernels for 2%

profile of v1, /device:TPU:4, one launch (start us, length us, event | category | flops | bytes accessed | tf_op | source)
XLA Modules:
  0.0 64.7 jit_solution(7211554605878719649)
XLA Ops:
  0.0 0.0 copy-start.1
  0.0 0.0 copy-start.8
  0.0 0.0 copy-start.7
  0.0 2.6 %shard_map.100 = (f32[4,256,256]{2,1,0:T(8,128)S(1)}, bf16[256,256]{1,0:T(8,128)(2,1)S(1)}, bf16[256,256]{1,0:T(8,128)(2,1)S(1)}, f32[2,256]{1,0:T(2,128)S(1)}) custom-call(s32[1]{0:T(128)} %bitcast.place.refs_0_, bf16[4,4,64,1024]{3,2,1,0:T(8,128)(2,1)} %refs_1_, bf16[1024,256]{1,0:T(8,128)(2,1)} %weight.1), custom_call_target="tpu_custom_call" | custom-call | flops 536870912 | bytes 1048576 | tf_op jit(solution)/shard_map/pallas_call | solution.py:188
  2.6 0.6 %broadcast_in_dim.9 = f32[32,1,2,256]{3,2,1,0:T(2,128)} broadcast(f32[2,256]{1,0:T(2,128)S(1)} %get-tuple-element.23), dimensions={2,3} | broadcast | bytes 67584 | tf_op jit(solution)/shard_map/broadcast_in_dim | solution.py:163
  3.2 12.9 %all-to-all-start = ((f32[32,1,2,256]{3,2,1,0:T(2,128)}), f32[32,1,2,256]{3,2,1,0:T(2,128)S(1)}, u32[]{:S(2)}, u32[]{:S(2)}) async-start(f32[32,1,2,256]{3,2,1,0:T(2,128)} %broadcast_in_dim.9), calls=%async_computation | async-start | bytes 131072 | tf_op jit(solution)/shard_map/all_to_all | solution.py:164
  16.1 3.7 %collective-permute-start = (bf16[256,256]{1,0:T(8,128)(2,1)S(1)}, bf16[256,256]{1,0:T(8,128)(2,1)S(1)}, u32[]{:S(2)}, u32[]{:S(2)}) collective-permute-start(bf16[256,256]{1,0:T(8,128)(2,1)S(1)} %get-tuple-element.26), channel_id=1, source_target_pairs={{0,1},{2,3},{4,5},{6,7},{8,9},{10,11},{12,13},{14,15},{16,17},{18,... | collective-permute-start | bytes 393224 | tf_op jit(solution)/shard_map/ppermute | solution.py:202
  19.9 0.7 %collective-permute-start.1 = (bf16[256,256]{1,0:T(8,128)(2,1)S(1)}, bf16[256,256]{1,0:T(8,128)(2,1)S(1)}, u32[]{:S(2)}, u32[]{:S(2)}) collective-permute-start(bf16[256,256]{1,0:T(8,128)(2,1)S(1)} %get-tuple-element.27), channel_id=1, source_target_pairs={{1,2},{3,4},{5,6},{7,8},{9,10},{11,12},{13,14},{15,16},{17,18},{19... | collective-permute-start | bytes 393224 | tf_op jit(solution)/shard_map/ppermute | solution.py:201
  20.5 5.9 %all-to-all-done = f32[32,1,2,256]{3,2,1,0:T(2,128)S(1)} async-done(((f32[32,1,2,256]{3,2,1,0:T(2,128)}), f32[32,1,2,256]{3,2,1,0:T(2,128)S(1)}, u32[]{:S(2)}, u32[]{:S(2)}) %all-to-all-start) | async-done | bytes 65568 | tf_op jit(solution)/shard_map/all_to_all | solution.py:164
  26.5 0.0 copy-done.1
  26.5 0.0 copy-done.8
  26.5 0.0 copy-done.7
  26.5 1.2 %shard_map.101 = (f32[4,256,256]{2,1,0:T(8,128)S(1)}, f32[2,8,256]{2,1,0:T(8,128)S(1)}, f32[3,256]{1,0:T(4,128)S(1)}) custom-call(f32[4,256,256]{2,1,0:T(8,128)S(1)} %get-tuple-element.21.refs_0_, f32[32,2,256]{2,1,0:T(2,128)S(1)} %bitcast.15, f32[1,256]{1,0:T(1,128)S(1)} %bitcast.20, f32[1,256]{1,0:T(1,128)S(1)} %bitcast.21, bf16[2304,256]{1,0:T(8,128)(2,1)S(1)} %bitcast.11), custom_call_target="tpu_custom_call" | custom-call | flops 1207959552 | bytes 1048576 | tf_op jit(solution)/shard_map/pallas_call | solution.py:207
  27.7 0.0 copy-start.2
  27.7 0.0 copy-start.5
  27.7 0.0 copy-start.6
  27.7 0.0 collective-permute-done.refs_2_
  27.7 0.0 collective-permute-done.1.refs_3_
  27.8 0.5 shard_map.102
  28.2 0.0 copy-start
  28.2 0.0 copy-start.3
  28.3 0.0 copy-start.4
  28.3 19.3 %all_to_all.15 = f32[32,1,2,256]{3,2,1,0:T(2,128)S(1)} all-to-all(f32[32,1,2,256]{3,2,1,0:T(2,128)S(1)} %broadcast_in_dim.10), channel_id=1, replica_groups=mesh['grp'=24,'bn'=32] {'bn'}, dimensions={0} | all-to-all | bytes 131072 | tf_op jit(solution)/shard_map/all_to_all | solution.py:164
  47.6 0.0 copy-done.2
  47.6 0.0 copy-done.5
  47.6 0.0 copy-done.6
  47.6 0.9 %shard_map.103 = (f32[4,256,1024]{2,1,0:T(8,128)S(1)}, f32[2,1024]{1,0:T(2,128)S(1)}) custom-call(f32[4,256,256]{2,1,0:T(8,128)S(1)} %get-tuple-element.25.refs_1_.refs_0_, f32[2,256,256]{2,1,0:T(8,128)S(1)} %get-tuple-element.30.refs_1_, f32[32,2,256]{2,1,0:T(2,128)S(1)} %bitcast.14, f32[1,256]{1,0:T(1,128)S(1)} %bitcast.18, f32[1,256]{1,0:T(1,128)S(1)} %bitcast.19, ...), custom_call_target="tpu_custom_call" | custom-call | flops 536870912 | bytes 1048576 | tf_op jit(solution)/shard_map/pallas_call | solution.py:230
  48.5 0.1 broadcast_in_dim.11
  48.6 14.2 %all_to_all.16 = f32[32,1,2,1024]{3,2,1,0:T(2,128)S(1)} all-to-all(f32[32,1,2,1024]{3,2,1,0:T(2,128)S(1)} %broadcast_in_dim.11), channel_id=1, replica_groups=mesh['grp'=24,'bn'=32] {'bn'}, dimensions={0} | all-to-all | bytes 524288 | tf_op jit(solution)/shard_map/all_to_all | solution.py:164
  62.8 0.0 copy-done
  62.8 0.0 copy-done.3
  62.8 0.0 copy-done.4
  62.8 1.8 %shard_map.104 = bf16[4,4,64,1024]{3,2,1,0:T(8,128)(2,1)} custom-call(f32[4,256,1024]{2,1,0:T(8,128)S(1)} %get-tuple-element.34.refs_0_, bf16[4,4,64,1024]{3,2,1,0:T(8,128)(2,1)S(1)} %copy-done, f32[32,2,1024]{2,1,0:T(2,128)S(1)} %bitcast.13, f32[1,1024]{1,0:T(1,128)S(1)} %bitcast.16, f32[1,1024]{1,0:T(1,128)S(1)} %bitcast.17), custom_call_target="tpu_custom_call" | custom-call | flops 8388608 | bytes 1048576 | tf_op jit(solution)/shard_map/pallas_call | solution.py:240
  (1 shorter events, 0.0 us)
Async XLA Ops:
  0.0 26.5 %copy-start.1 = (bf16[3,3,256,256]{3,2,1,0:T(8,128)(2,1)S(1)}, bf16[3,3,256,256]{3,2,1,0:T(8,128)(2,1)}, u32[]{:S(2)}) copy-start(bf16[3,3,256,256]{3,2,1,0:T(8,128)(2,1)} %param.12) | copy-start | bytes 3538948
  0.0 26.5 %copy-start.8 = (f32[256]{0:T(256)S(1)}, f32[256]{0:T(256)}, u32[]{:S(2)}) copy-start(f32[256]{0:T(256)} %param.15) | copy-start | bytes 3076
  0.0 26.5 %copy-start.7 = (f32[256]{0:T(256)S(1)}, f32[256]{0:T(256)}, u32[]{:S(2)}) copy-start(f32[256]{0:T(256)} %param.14) | copy-start | bytes 3076
  3.2 23.2 %all-to-all-start = ((f32[32,1,2,256]{3,2,1,0:T(2,128)}), f32[32,1,2,256]{3,2,1,0:T(2,128)S(1)}, u32[]{:S(2)}, u32[]{:S(2)}) async-start(f32[32,1,2,256]{3,2,1,0:T(2,128)} %broadcast_in_dim.9), calls=%async_computation | async-start | bytes 131072 | tf_op jit(solution)/shard_map/all_to_all | solution.py:164
  16.1 11.6 %collective-permute-start = (bf16[256,256]{1,0:T(8,128)(2,1)S(1)}, bf16[256,256]{1,0:T(8,128)(2,1)S(1)}, u32[]{:S(2)}, u32[]{:S(2)}) collective-permute-start(bf16[256,256]{1,0:T(8,128)(2,1)S(1)} %get-tuple-element.26), channel_id=1, source_target_pairs={{0,1},{2,3},{4,5},{6,7},{8,9},{10,11},{12,13},{14,15},{16,17},{18,... | collective-permute-start | bytes 393224 | tf_op jit(solution)/shard_map/ppermute | solution.py:202
  19.9 7.9 %collective-permute-start.1 = (bf16[256,256]{1,0:T(8,128)(2,1)S(1)}, bf16[256,256]{1,0:T(8,128)(2,1)S(1)}, u32[]{:S(2)}, u32[]{:S(2)}) collective-permute-start(bf16[256,256]{1,0:T(8,128)(2,1)S(1)} %get-tuple-element.27), channel_id=1, source_target_pairs={{1,2},{3,4},{5,6},{7,8},{9,10},{11,12},{13,14},{15,16},{17,18},{19... | collective-permute-start | bytes 393224 | tf_op jit(solution)/shard_map/ppermute | solution.py:201
  27.7 19.9 %copy-start.2 = (bf16[256,1024]{1,0:T(8,128)(2,1)S(1)}, bf16[256,1024]{1,0:T(8,128)(2,1)}, u32[]{:S(2)}) copy-start(bf16[256,1024]{1,0:T(8,128)(2,1)} %refs_5_) | copy-start | bytes 1572868
  27.7 19.9 %copy-start.5 = (f32[256]{0:T(256)S(1)}, f32[256]{0:T(256)}, u32[]{:S(2)}) copy-start(f32[256]{0:T(256)} %param.16) | copy-start | bytes 3076
  27.7 19.9 %copy-start.6 = (f32[256]{0:T(256)S(1)}, f32[256]{0:T(256)}, u32[]{:S(2)}) copy-start(f32[256]{0:T(256)} %param.17) | copy-start | bytes 3076
  28.2 34.6 %copy-start = (bf16[4,4,64,1024]{3,2,1,0:T(8,128)(2,1)S(1)}, bf16[4,4,64,1024]{3,2,1,0:T(8,128)(2,1)}, u32[]{:S(2)}) copy-start(bf16[4,4,64,1024]{3,2,1,0:T(8,128)(2,1)} %refs_1_) | copy-start | bytes 6291460
  28.2 34.6 %copy-start.3 = (f32[1024]{0:T(1024)S(1)}, f32[1024]{0:T(1024)}, u32[]{:S(2)}) copy-start(f32[1024]{0:T(1024)} %param.18) | copy-start | bytes 12292
  28.3 34.6 %copy-start.4 = (f32[1024]{0:T(1024)S(1)}, f32[1024]{0:T(1024)}, u32[]{:S(2)}) copy-start(f32[1024]{0:T(1024)} %param.19) | copy-start | bytes 12292

commit v2 on v1

--- a/solution.py
+++ b/solution.py
@@ -6,6 +6,8 @@
 from jax.sharding import PartitionSpec as P
 
 epsilon = 1e-05
+LEADS0 = (4, 5, 5)
+LEADS = (5, 5, 5)
 f32 = jnp.float32
 bf16 = jnp.bfloat16
 
@@ -128,24 +130,45 @@
 def expand_kernel(population, mid, edge, gathered, gain, shift, weight, last, sums):
     rows = mid.shape[0]
     average, factor, bias = factors(gathered, gain, shift, population)
+    c = weight.shape[0]
     total = squares = None
     for r in range(rows):
         value = edge[0] if r == 0 else edge[1] if r == rows - 1 else mid[r]
         hidden = jnp.maximum((value - average) * factor + bias, 0.0).astype(bf16)
         y = jnp.dot(hidden, weight[...], preferred_element_type=f32)
         last[r] = y
-        a, b = eights(y), eights(y * y)
+        a, b = eights(hidden.astype(f32)), eights(y * y)
         total, squares = (a, b) if r == 0 else (total + a, squares + b)
-    store_sums(sums, total, squares)
-
-
-def final_kernel(population, last, images, gathered, gain, shift, out, staged, sem):
+    squares = jnp.sum(squares, axis=0, keepdims=True)
+    half = sums.shape[1]
+    sums[0:1, 0:c] = jnp.sum(total, axis=0, keepdims=True)
+    sums[0:1, c:half] = squares[:, : half - c]
+    sums[1:2, :] = squares[:, half - c :]
+
+
+def times(row, weight):
+    high = row.astype(bf16).astype(f32)
+    mid = (row - high).astype(bf16).astype(f32)
+    low = (row - high - mid).astype(bf16).astype(f32)
+    place = lax.broadcasted_iota(jnp.int32, (8, row.shape[1]), 0)
+    pieces = jnp.where(place == 0, high, jnp.where(place == 1, mid, jnp.where(place == 2, low, 0.0)))
+    product = jnp.dot(pieces.astype(bf16), weight, preferred_element_type=f32)
+    return jnp.sum(product, axis=0, keepdims=True)
+
+
+def final_kernel(population, last, images, gathered, gain, shift, weight, out, staged, sem):
     imgs, rows, wid, _ = images.shape
-    average, factor, bias = factors(gathered, gain, shift, population)
+    c = weight.shape[0]
+    sums = jnp.sum(gathered[...], axis=0)
+    average = times(sums[0:1, :c] / population, weight[...])
+    squares = jnp.concatenate([sums[0:1, c:], sums[1:2, :]], axis=1)
+    spread = squares / population - average * average
+    factor = gain[...] * lax.rsqrt(spread + epsilon)
+    bias = shift[...] - average * factor
     copies = []
     for n in range(imgs):
         for r in range(rows):
-            value = (last[r, n * wid : (n + 1) * wid, :] - average) * factor + bias
+            value = last[r, n * wid : (n + 1) * wid, :] * factor + bias
             value = value + images[n, r].astype(f32)
             staged[n, r] = jnp.maximum(value, 0.0).astype(bf16)
             copies.append(pltpu.make_async_copy(staged.at[n, r], out.at[n, r], sem.at[n, r]))
@@ -159,9 +182,16 @@
     return [(i, i + 1) for i in firsts] + [(i + 1, i) for i in firsts]
 
 
-def to_all(sums, count):
+def to_all(sums, heads):
+    count = lax.axis_size("bn")
+    groups = [
+        [g * count + i for i in [head] + [i for i in range(count) if i != head]]
+        for g, head in enumerate(heads)
+    ]
     copies = jnp.broadcast_to(sums, (count, 1, *sums.shape))
-    got = lax.all_to_all(copies, "bn", split_axis=0, concat_axis=0, tiled=True)
+    got = lax.all_to_all(
+        copies, ("grp", "bn"), split_axis=0, concat_axis=0, tiled=True, axis_index_groups=groups
+    )
     return in_vmem(got.reshape(count, *sums.shape))
 
 
@@ -181,6 +211,8 @@
     imgs, rows, wid, ch = images.shape
     mid_ch = w_reduce.shape[1]
     cells = imgs * wid
+    eighth = count // 8
+    heads = lambda i: [LEADS0[i - 1] * eighth] + [LEADS[i - 1] * eighth] * (lax.axis_size("grp") - 1)
     population = float(cells * rows * count)
     row = lambda v: in_vmem(v.reshape(1, -1))
 
@@ -202,7 +234,7 @@
     near = lax.ppermute(near, "bn", pairs(0, count))
 
     w_spatial, sums = lax.optimization_barrier((w_spatial, sums))
-    gathered = to_all(sums, count)
+    gathered = to_all(sums, heads(1))
     weight = in_vmem(w_spatial.reshape(-1, mid_ch))
     middle, inner, norm = call(
         lambda *refs: inner_kernel(wid, population, *refs),
@@ -225,26 +257,27 @@
         2 * cells * 6 * mid_ch * mid_ch,
     )(place, middle, in_vmem(near), in_vmem(far), norm, weight, inner)
     images, w_expand, sums = lax.optimization_barrier((images, w_expand, sums))
-    gathered = to_all(sums, count)
-
+    gathered = to_all(sums, heads(2))
+
+    expand = in_vmem(w_expand)
     last, sums = call(
         lambda *refs: expand_kernel(population, *refs),
-        [pltpu.VMEM((rows, cells, ch), f32), pltpu.VMEM((2, ch), f32)],
+        [pltpu.VMEM((rows, cells, ch), f32), pltpu.VMEM((2, (mid_ch + ch) // 2), f32)],
         [VM] * 6,
         [VM] * 2,
         (),
         2 * cells * rows * ch * mid_ch,
-    )(middle, edge, gathered, row(gain_middle), row(shift_middle), in_vmem(w_expand))
-    gathered = to_all(sums, count)
+    )(middle, edge, gathered, row(gain_middle), row(shift_middle), expand)
+    gathered = to_all(sums, heads(3))
 
     return call(
         lambda *refs: final_kernel(population, *refs),
         jax.ShapeDtypeStruct(images.shape, bf16),
-        [VM] * 5,
+        [VM] * 6,
         HB,
         [pltpu.VMEM(images.shape, bf16), pltpu.SemaphoreType.DMA((imgs, rows))],
         8 * cells * rows * ch,
-    )(last, in_vmem(images), gathered, row(gain_last), row(shift_last))
+    )(last, in_vmem(images), gathered, row(gain_last), row(shift_last), expand)
 
 
 def solution(mesh):

time: 64.9 us -> 58.8 us (0.906)
  the two profiles are of different devices: /device:TPU:4 before, /device:TPU:8 now
where the time goes in v2:
time: 58.8 us; the launch traced here: 58.6 us
  blocking collectives  28.9 us (49%)
  starting transfers between devices  20 us (34%)
  Pallas kernels  7.16 us (12%)
  waiting for transfers between devices  1.64 us (3%)
  local copies, waits for them, and re-layouts  0.75 us (1%)
    all_to_all x2, blocking collectives, to_all(): lax.all_to_all(copies, ('grp', 'bn'), split_axis=0, concat_axis=0, tiled=...  28.9 us
    all_to_all x1, starting transfers between devices, to_all(): lax.all_to_all(copies, ('grp', 'bn'), split_axis=0, concat_axis=0, tiled=...  13.2 us
    ppermute x1, starting transfers between devices, body(): far = lax.ppermute(far, 'bn', pairs(1, count))  4.27 us
    pallas_call x1, Pallas kernels, body(): call(reduce_kernel, [pltpu.VMEM((rows, cells, mid_ch), f32), pltpu.VMEM((...  2.55 us
    ppermute x1, starting transfers between devices, body(): near = lax.ppermute(near, 'bn', pairs(0, count))  2.47 us
    pallas_call x1, Pallas kernels, body(): call(lambda *refs: final_kernel(population, *refs), jax.ShapeDtypeStruct(...  2.09 us
    pallas_call x1, Pallas kernels, body(): call(lambda *refs: inner_kernel(wid, population, *refs), [pltpu.VMEM((row...  1.23 us
  transfers between devices with their start and end apart: 3, of which 2 were waited for; matrix products, arithmetic and copies ran while one was open for 0% of the time, Pallas kernels for 2%

profile of v2, /device:TPU:8, one launch (start us, length us, event | category | flops | bytes accessed | tf_op | source)
XLA Modules:
  0.0 58.6 jit_solution(16856684791613982578)
XLA Ops:
  0.0 0.0 copy-start.2
  0.0 0.0 copy-start.8
  0.0 0.0 copy-start.7
  0.0 2.6 %shard_map.100 = (f32[4,256,256]{2,1,0:T(8,128)S(1)}, bf16[256,256]{1,0:T(8,128)(2,1)S(1)}, bf16[256,256]{1,0:T(8,128)(2,1)S(1)}, f32[2,256]{1,0:T(2,128)S(1)}) custom-call(s32[1]{0:T(128)} %bitcast.place.refs_0_, bf16[4,4,64,1024]{3,2,1,0:T(8,128)(2,1)} %refs_1_, bf16[1024,256]{1,0:T(8,128)(2,1)} %weight.1), custom_call_target="tpu_custom_call" | custom-call | flops 536870912 | bytes 1048576 | tf_op jit(solution)/shard_map/pallas_call | solution.py:220
  2.6 0.6 %broadcast_in_dim.9 = f32[32,1,2,256]{3,2,1,0:T(2,128)} broadcast(f32[2,256]{1,0:T(2,128)S(1)} %get-tuple-element.23), dimensions={2,3} | broadcast | bytes 67584 | tf_op jit(solution)/shard_map/broadcast_in_dim | solution.py:191
  3.2 13.2 %all-to-all-start = ((f32[32,1,2,256]{3,2,1,0:T(2,128)}), f32[32,1,2,256]{3,2,1,0:T(2,128)S(1)}, u32[]{:S(2)}, u32[]{:S(2)}) async-start(f32[32,1,2,256]{3,2,1,0:T(2,128)} %broadcast_in_dim.9), calls=%async_computation | async-start | bytes 131072 | tf_op jit(solution)/shard_map/all_to_all | solution.py:192
  16.4 2.5 %collective-permute-start = (bf16[256,256]{1,0:T(8,128)(2,1)S(1)}, bf16[256,256]{1,0:T(8,128)(2,1)S(1)}, u32[]{:S(2)}, u32[]{:S(2)}) collective-permute-start(bf16[256,256]{1,0:T(8,128)(2,1)S(1)} %get-tuple-element.26), channel_id=1, source_target_pairs={{0,1},{2,3},{4,5},{6,7},{8,9},{10,11},{12,13},{14,15},{16,17},{18,... | collective-permute-start | bytes 393224 | tf_op jit(solution)/shard_map/ppermute | solution.py:234
  18.9 4.3 %collective-permute-start.1 = (bf16[256,256]{1,0:T(8,128)(2,1)S(1)}, bf16[256,256]{1,0:T(8,128)(2,1)S(1)}, u32[]{:S(2)}, u32[]{:S(2)}) collective-permute-start(bf16[256,256]{1,0:T(8,128)(2,1)S(1)} %get-tuple-element.27), channel_id=1, source_target_pairs={{1,2},{3,4},{5,6},{7,8},{9,10},{11,12},{13,14},{15,16},{17,18},{19... | collective-permute-start | bytes 393224 | tf_op jit(solution)/shard_map/ppermute | solution.py:233
  23.2 0.7 %all-to-all-done = f32[32,1,2,256]{3,2,1,0:T(2,128)S(1)} async-done(((f32[32,1,2,256]{3,2,1,0:T(2,128)}), f32[32,1,2,256]{3,2,1,0:T(2,128)S(1)}, u32[]{:S(2)}, u32[]{:S(2)}) %all-to-all-start) | async-done | bytes 65568 | tf_op jit(solution)/shard_map/all_to_all | solution.py:192
  23.9 0.0 copy-done.2
  23.9 0.0 copy-done.8
  23.9 0.0 copy-done.7
  23.9 1.2 %shard_map.101 = (f32[4,256,256]{2,1,0:T(8,128)S(1)}, f32[2,8,256]{2,1,0:T(8,128)S(1)}, f32[3,256]{1,0:T(4,128)S(1)}) custom-call(f32[4,256,256]{2,1,0:T(8,128)S(1)} %get-tuple-element.21.refs_0_, f32[32,2,256]{2,1,0:T(2,128)S(1)} %bitcast.15, f32[1,256]{1,0:T(1,128)S(1)} %bitcast.20, f32[1,256]{1,0:T(1,128)S(1)} %bitcast.21, bf16[2304,256]{1,0:T(8,128)(2,1)S(1)} %bitcast.11), custom_call_target="tpu_custom_call" | custom-call | flops 1207959552 | bytes 1048576 | tf_op jit(solution)/shard_map/pallas_call | solution.py:239
  25.2 0.0 copy-start.1
  25.2 0.0 copy-start.5
  25.2 0.0 copy-start.6
  25.2 0.0 collective-permute-done.refs_2_
  25.2 0.9 %collective-permute-done.1.refs_3_ = bf16[256,256]{1,0:T(8,128)(2,1)S(1)} collective-permute-done((bf16[256,256]{1,0:T(8,128)(2,1)S(1)}, bf16[256,256]{1,0:T(8,128)(2,1)S(1)}, u32[]{:S(2)}, u32[]{:S(2)}) %collective-permute-start.1) | collective-permute-done | bytes 131104 | tf_op jit(solution)/shard_map/ppermute | solution.py:233
  26.1 0.0 copy-start
  26.1 0.0 copy-start.3
  26.1 0.0 copy-start.4
  26.1 0.5 shard_map.102
  26.6 15.5 %all_to_all.15 = f32[32,1,2,256]{3,2,1,0:T(2,128)S(1)} all-to-all(f32[32,1,2,256]{3,2,1,0:T(2,128)S(1)} %broadcast_in_dim.10), channel_id=1, replica_groups={{20,0,1,2,3,4,5,6,7,8,9,10,11,12,13,14,15,16,17,18,19,21,22,23,24,25,26..., dimensions={0} | all-to-all | bytes 131072 | tf_op jit(solution)/shard_map/all_to_all | solution.py:192
  42.1 0.0 copy-done.1
  42.1 0.0 copy-done.5
  42.1 0.0 copy-done.6
  42.1 0.8 %shard_map.103 = (f32[4,256,1024]{2,1,0:T(8,128)S(1)}, f32[2,640]{1,0:T(2,128)S(1)}) custom-call(f32[4,256,256]{2,1,0:T(8,128)S(1)} %get-tuple-element.25.refs_1_.refs_0_, f32[2,256,256]{2,1,0:T(8,128)S(1)} %get-tuple-element.30.refs_1_, f32[32,2,256]{2,1,0:T(2,128)S(1)} %bitcast.14, f32[1,256]{1,0:T(1,128)S(1)} %bitcast.18, f32[1,256]{1,0:T(1,128)S(1)} %bitcast.19, ...), custom_call_target="tpu_custom_call" | custom-call | flops 536870912 | bytes 1048576 | tf_op jit(solution)/shard_map/pallas_call | solution.py:263
  43.0 13.5 %all_to_all.16 = f32[32,1,2,640]{3,2,1,0:T(2,128)S(1)} all-to-all(f32[32,1,2,640]{3,2,1,0:T(2,128)S(1)} %broadcast_in_dim.11), channel_id=1, replica_groups={{20,0,1,2,3,4,5,6,7,8,9,10,11,12,13,14,15,16,17,18,19,21,22,23,24,25,26..., dimensions={0} | all-to-all | bytes 327680 | tf_op jit(solution)/shard_map/all_to_all | solution.py:192
  56.5 0.0 copy-done
  56.5 0.0 copy-done.3
  56.5 0.0 copy-done.4
  56.5 2.1 %shard_map.104 = bf16[4,4,64,1024]{3,2,1,0:T(8,128)(2,1)} custom-call(f32[4,256,1024]{2,1,0:T(8,128)S(1)} %get-tuple-element.34.refs_0_, bf16[4,4,64,1024]{3,2,1,0:T(8,128)(2,1)S(1)} %copy-done, f32[32,2,640]{2,1,0:T(2,128)S(1)} %bitcast.13, f32[1,1024]{1,0:T(1,128)S(1)} %bitcast.16, f32[1,1024]{1,0:T(1,128)S(1)} %bitcast.17, bf16[256,1024]{1,0:T(8,128)(2,1)S(1)} %copy-done.1), custom_call_target="tpu_custom_call" | custom-call | flops 8388608 | bytes 1048576 | tf_op jit(solution)/shard_map/pallas_call | solution.py:273
  (2 shorter events, 0.1 us)
Async XLA Ops:
  0.0 23.9 %copy-start.2 = (bf16[3,3,256,256]{3,2,1,0:T(8,128)(2,1)S(1)}, bf16[3,3,256,256]{3,2,1,0:T(8,128)(2,1)}, u32[]{:S(2)}) copy-start(bf16[3,3,256,256]{3,2,1,0:T(8,128)(2,1)} %param.12) | copy-start | bytes 3538948
  0.0 23.9 %copy-start.8 = (f32[256]{0:T(256)S(1)}, f32[256]{0:T(256)}, u32[]{:S(2)}) copy-start(f32[256]{0:T(256)} %param.15) | copy-start | bytes 3076
  0.0 23.9 %copy-start.7 = (f32[256]{0:T(256)S(1)}, f32[256]{0:T(256)}, u32[]{:S(2)}) copy-start(f32[256]{0:T(256)} %param.14) | copy-start | bytes 3076
  3.2 20.7 %all-to-all-start = ((f32[32,1,2,256]{3,2,1,0:T(2,128)}), f32[32,1,2,256]{3,2,1,0:T(2,128)S(1)}, u32[]{:S(2)}, u32[]{:S(2)}) async-start(f32[32,1,2,256]{3,2,1,0:T(2,128)} %broadcast_in_dim.9), calls=%async_computation | async-start | bytes 131072 | tf_op jit(solution)/shard_map/all_to_all | solution.py:192
  16.4 8.7 %collective-permute-start = (bf16[256,256]{1,0:T(8,128)(2,1)S(1)}, bf16[256,256]{1,0:T(8,128)(2,1)S(1)}, u32[]{:S(2)}, u32[]{:S(2)}) collective-permute-start(bf16[256,256]{1,0:T(8,128)(2,1)S(1)} %get-tuple-element.26), channel_id=1, source_target_pairs={{0,1},{2,3},{4,5},{6,7},{8,9},{10,11},{12,13},{14,15},{16,17},{18,... | collective-permute-start | bytes 393224 | tf_op jit(solution)/shard_map/ppermute | solution.py:234
  18.9 7.2 %collective-permute-start.1 = (bf16[256,256]{1,0:T(8,128)(2,1)S(1)}, bf16[256,256]{1,0:T(8,128)(2,1)S(1)}, u32[]{:S(2)}, u32[]{:S(2)}) collective-permute-start(bf16[256,256]{1,0:T(8,128)(2,1)S(1)} %get-tuple-element.27), channel_id=1, source_target_pairs={{1,2},{3,4},{5,6},{7,8},{9,10},{11,12},{13,14},{15,16},{17,18},{19... | collective-permute-start | bytes 393224 | tf_op jit(solution)/shard_map/ppermute | solution.py:233
  25.2 17.0 %copy-start.1 = (bf16[256,1024]{1,0:T(8,128)(2,1)S(1)}, bf16[256,1024]{1,0:T(8,128)(2,1)}, u32[]{:S(2)}) copy-start(bf16[256,1024]{1,0:T(8,128)(2,1)} %refs_5_.1) | copy-start | bytes 1572868
  25.2 16.9 %copy-start.5 = (f32[256]{0:T(256)S(1)}, f32[256]{0:T(256)}, u32[]{:S(2)}) copy-start(f32[256]{0:T(256)} %param.16) | copy-start | bytes 3076
  25.2 16.9 %copy-start.6 = (f32[256]{0:T(256)S(1)}, f32[256]{0:T(256)}, u32[]{:S(2)}) copy-start(f32[256]{0:T(256)} %param.17) | copy-start | bytes 3076
  26.1 30.3 %copy-start = (bf16[4,4,64,1024]{3,2,1,0:T(8,128)(2,1)S(1)}, bf16[4,4,64,1024]{3,2,1,0:T(8,128)(2,1)}, u32[]{:S(2)}) copy-start(bf16[4,4,64,1024]{3,2,1,0:T(8,128)(2,1)} %refs_1_) | copy-start | bytes 6291460
  26.1 30.3 %copy-start.3 = (f32[1024]{0:T(1024)S(1)}, f32[1024]{0:T(1024)}, u32[]{:S(2)}) copy-start(f32[1024]{0:T(1024)} %param.18) | copy-start | bytes 12292
  26.1 30.3 %copy-start.4 = (f32[1024]{0:T(1024)S(1)}, f32[1024]{0:T(1024)}, u32[]{:S(2)}) copy-start(f32[1024]{0:T(1024)} %param.19) | copy-start | bytes 12292

commit v3 on v2

--- a/solution.py
+++ b/solution.py
@@ -67,12 +67,13 @@
         y = jnp.dot(x, w_vmem[...], preferred_element_type=f32)
         for r in range(rows):
             first[r, n * wid : (n + 1) * wid, :] = y[r * wid : (r + 1) * wid]
-        head, tail = y[:wid].astype(bf16), y[(rows - 1) * wid :].astype(bf16)
-        near[n * wid : (n + 1) * wid, :] = jnp.where(even, tail, head)
-        far[n * wid : (n + 1) * wid, :] = jnp.where(even, head, tail)
         a, b = eights(y), eights(y * y)
         total, squares = (a, b) if n == 0 else (total + a, squares + b)
     store_sums(sums, total, squares)
+    own = sums[0:1, :] / float(imgs * rows * wid)
+    head, tail = (first[0] - own).astype(bf16), (first[rows - 1] - own).astype(bf16)
+    near[...] = jnp.where(even, tail, head)
+    far[...] = jnp.where(even, head, tail)
 
 
 def spread_columns(hidden, out, wid):
@@ -108,12 +109,16 @@
     sums[1] = squares
 
 
-def edge_kernel(wid, ends, place, mid, near, far, norm, weight, inner, edge, sums, cells):
+def edge_kernel(wid, ends, heads, place, part, mid, near, far, gathered, norm, weight, inner, edge, sums, cells):
     rows = mid.shape[0]
     k = cells.shape[2]
     even = place[0] % 2 == 0
+    leader = jnp.where(part[0] == 0, heads[0], heads[1])
     for i in range(2):
-        halo = jnp.where(even == (i == 0), far[...], near[...]).astype(f32)
+        sender = jnp.clip(place[0] + 2 * i - 1, 0, ends)
+        slot = jnp.where(sender == leader, 0, jnp.where(sender < leader, sender + 1, sender))
+        shift = gathered[pl.ds(slot, 1)][0, 0:1, :] / float(rows * mid.shape[1])
+        halo = jnp.where(even == (i == 0), far[...], near[...]).astype(f32) + shift
         hidden = jnp.maximum((halo - norm[0:1, :]) * norm[1:2, :] + norm[2:3, :], 0.0)
         hidden = jnp.where(place[0] == (0 if i == 0 else ends), 0.0, hidden)
         spread_columns(hidden, cells.at[i], wid)
@@ -213,10 +218,11 @@
     cells = imgs * wid
     eighth = count // 8
     heads = lambda i: [LEADS0[i - 1] * eighth] + [LEADS[i - 1] * eighth] * (lax.axis_size("grp") - 1)
+    place, part = (lax.axis_index(a).astype(jnp.int32).reshape(1) for a in ("bn", "grp"))
+    first_heads = heads(1)[0], heads(1)[-1]
     population = float(cells * rows * count)
     row = lambda v: in_vmem(v.reshape(1, -1))
 
-    place = lax.axis_index("bn").astype(jnp.int32).reshape(1)
     first, near, far, sums = call(
         reduce_kernel,
         [
@@ -249,13 +255,13 @@
         2 * cells * rows * 9 * mid_ch * mid_ch,
     )(first, gathered, row(gain_first), row(shift_first), weight)
     edge, sums = call(
-        lambda *refs: edge_kernel(wid, count - 1, *refs),
+        lambda *refs: edge_kernel(wid, count - 1, first_heads, *refs),
         [pltpu.VMEM((2, cells, mid_ch), f32), pltpu.VMEM((2, mid_ch), f32)],
-        [SM] + [VM] * 6,
+        [SM] * 2 + [VM] * 7,
         [VM] * 2,
         [pltpu.VMEM((2, cells, 3 * mid_ch), bf16)],
         2 * cells * 6 * mid_ch * mid_ch,
-    )(place, middle, in_vmem(near), in_vmem(far), norm, weight, inner)
+    )(place, part, middle, in_vmem(near), in_vmem(far), gathered, norm, weight, inner)
     images, w_expand, sums = lax.optimization_barrier((images, w_expand, sums))
     gathered = to_all(sums, heads(2))
 

time: 58.8 us -> 58.9 us (level)
  no operation moved by 1% of the time
where the time goes in v3:
time: 58.9 us; the launch traced here: 58.6 us
  blocking collectives  28.9 us (49%)
  starting transfers between devices  20 us (34%)
  Pallas kernels  7.2 us (12%)
  waiting for transfers between devices  1.63 us (3%)
  local copies, waits for them, and re-layouts  0.75 us (1%)
    all_to_all x2, blocking collectives, to_all(): lax.all_to_all(copies, ('grp', 'bn'), split_axis=0, concat_axis=0, tiled=...  28.9 us
    all_to_all x1, starting transfers between devices, to_all(): lax.all_to_all(copies, ('grp', 'bn'), split_axis=0, concat_axis=0, tiled=...  13.2 us
    ppermute x1, starting transfers between devices, body(): far = lax.ppermute(far, 'bn', pairs(1, count))  4.27 us
    pallas_call x1, Pallas kernels, body(): call(reduce_kernel, [pltpu.VMEM((rows, cells, mid_ch), f32), pltpu.VMEM((...  2.6 us
    ppermute x1, starting transfers between devices, body(): near = lax.ppermute(near, 'bn', pairs(0, count))  2.47 us
    pallas_call x1, Pallas kernels, body(): call(lambda *refs: final_kernel(population, *refs), jax.ShapeDtypeStruct(...  2.09 us
    pallas_call x1, Pallas kernels, body(): call(lambda *refs: inner_kernel(wid, population, *refs), [pltpu.VMEM((row...  1.23 us
  transfers between devices with their start and end apart: 3, of which 2 were waited for; matrix products, arithmetic and copies ran while one was open for 0% of the time, Pallas kernels for 2%

profile of v3, /device:TPU:8, one launch (start us, length us, event | category | flops | bytes accessed | tf_op | source)
XLA Modules:
  0.0 58.6 jit_solution(14170402800676379081)
XLA Ops:
  0.0 0.0 copy-start.2
  0.0 0.0 copy-start.8
  0.0 0.0 copy-start.7
  0.0 2.6 %shard_map.100 = (f32[4,256,256]{2,1,0:T(8,128)S(1)}, bf16[256,256]{1,0:T(8,128)(2,1)S(1)}, bf16[256,256]{1,0:T(8,128)(2,1)S(1)}, f32[2,256]{1,0:T(2,128)S(1)}) custom-call(s32[1]{0:T(128)} %bitcast.place.refs_0_, bf16[4,4,64,1024]{3,2,1,0:T(8,128)(2,1)} %refs_1_, bf16[1024,256]{1,0:T(8,128)(2,1)} %weight.1), custom_call_target="tpu_custom_call" | custom-call | flops 536870912 | bytes 1048576 | tf_op jit(solution)/shard_map/pallas_call | solution.py:226
  2.6 0.6 %broadcast_in_dim.9 = f32[32,1,2,256]{3,2,1,0:T(2,128)} broadcast(f32[2,256]{1,0:T(2,128)S(1)} %get-tuple-element.23), dimensions={2,3} | broadcast | bytes 67584 | tf_op jit(solution)/shard_map/broadcast_in_dim | solution.py:196
  3.3 13.2 %all-to-all-start = ((f32[32,1,2,256]{3,2,1,0:T(2,128)}), f32[32,1,2,256]{3,2,1,0:T(2,128)S(1)}, u32[]{:S(2)}, u32[]{:S(2)}) async-start(f32[32,1,2,256]{3,2,1,0:T(2,128)} %broadcast_in_dim.9), calls=%async_computation | async-start | bytes 131072 | tf_op jit(solution)/shard_map/all_to_all | solution.py:197
  16.5 2.5 %collective-permute-start = (bf16[256,256]{1,0:T(8,128)(2,1)S(1)}, bf16[256,256]{1,0:T(8,128)(2,1)S(1)}, u32[]{:S(2)}, u32[]{:S(2)}) collective-permute-start(bf16[256,256]{1,0:T(8,128)(2,1)S(1)} %get-tuple-element.26), channel_id=1, source_target_pairs={{0,1},{2,3},{4,5},{6,7},{8,9},{10,11},{12,13},{14,15},{16,17},{18,... | collective-permute-start | bytes 393224 | tf_op jit(solution)/shard_map/ppermute | solution.py:240
  19.0 4.3 %collective-permute-start.1 = (bf16[256,256]{1,0:T(8,128)(2,1)S(1)}, bf16[256,256]{1,0:T(8,128)(2,1)S(1)}, u32[]{:S(2)}, u32[]{:S(2)}) collective-permute-start(bf16[256,256]{1,0:T(8,128)(2,1)S(1)} %get-tuple-element.27), channel_id=1, source_target_pairs={{1,2},{3,4},{5,6},{7,8},{9,10},{11,12},{13,14},{15,16},{17,18},{19... | collective-permute-start | bytes 393224 | tf_op jit(solution)/shard_map/ppermute | solution.py:239
  23.3 0.7 %all-to-all-done = f32[32,1,2,256]{3,2,1,0:T(2,128)S(1)} async-done(((f32[32,1,2,256]{3,2,1,0:T(2,128)}), f32[32,1,2,256]{3,2,1,0:T(2,128)S(1)}, u32[]{:S(2)}, u32[]{:S(2)}) %all-to-all-start) | async-done | bytes 65568 | tf_op jit(solution)/shard_map/all_to_all | solution.py:197
  24.0 0.0 copy-done.2
  24.0 0.0 copy-done.8
  24.0 0.0 copy-done.7
  24.0 1.2 %shard_map.101 = (f32[4,256,256]{2,1,0:T(8,128)S(1)}, f32[2,8,256]{2,1,0:T(8,128)S(1)}, f32[3,256]{1,0:T(4,128)S(1)}) custom-call(f32[4,256,256]{2,1,0:T(8,128)S(1)} %get-tuple-element.21.refs_0_, f32[32,2,256]{2,1,0:T(2,128)S(1)} %bitcast.15, f32[1,256]{1,0:T(1,128)S(1)} %bitcast.22, f32[1,256]{1,0:T(1,128)S(1)} %bitcast.23, bf16[2304,256]{1,0:T(8,128)(2,1)S(1)} %bitcast.12), custom_call_target="tpu_custom_call" | custom-call | flops 1207959552 | bytes 1048576 | tf_op jit(solution)/shard_map/pallas_call | solution.py:245
  25.2 0.0 copy-start.1
  25.2 0.0 copy-start.5
  25.2 0.0 copy-start.6
  25.2 0.0 collective-permute-done.refs_3_
  25.2 0.9 %collective-permute-done.1.refs_4_ = bf16[256,256]{1,0:T(8,128)(2,1)S(1)} collective-permute-done((bf16[256,256]{1,0:T(8,128)(2,1)S(1)}, bf16[256,256]{1,0:T(8,128)(2,1)S(1)}, u32[]{:S(2)}, u32[]{:S(2)}) %collective-permute-start.1) | collective-permute-done | bytes 131104 | tf_op jit(solution)/shard_map/ppermute | solution.py:239
  26.2 0.0 copy-start
  26.2 0.0 copy-start.3
  26.2 0.0 copy-start.4
  26.2 0.5 shard_map.102
  26.7 15.5 %all_to_all.15 = f32[32,1,2,256]{3,2,1,0:T(2,128)S(1)} all-to-all(f32[32,1,2,256]{3,2,1,0:T(2,128)S(1)} %broadcast_in_dim.10), channel_id=1, replica_groups={{20,0,1,2,3,4,5,6,7,8,9,10,11,12,13,14,15,16,17,18,19,21,22,23,24,25,26..., dimensions={0} | all-to-all | bytes 131072 | tf_op jit(solution)/shard_map/all_to_all | solution.py:197
  42.2 0.0 copy-done.1
  42.2 0.0 copy-done.5
  42.2 0.0 copy-done.6
  42.2 0.8 %shard_map.103 = (f32[4,256,1024]{2,1,0:T(8,128)S(1)}, f32[2,640]{1,0:T(2,128)S(1)}) custom-call(f32[4,256,256]{2,1,0:T(8,128)S(1)} %get-tuple-element.25.refs_2_.refs_0_, f32[2,256,256]{2,1,0:T(8,128)S(1)} %get-tuple-element.30.refs_1_, f32[32,2,256]{2,1,0:T(2,128)S(1)} %bitcast.17, f32[1,256]{1,0:T(1,128)S(1)} %bitcast.20, f32[1,256]{1,0:T(1,128)S(1)} %bitcast.21, ...), custom_call_target="tpu_custom_call" | custom-call | flops 536870912 | bytes 1048576 | tf_op jit(solution)/shard_map/pallas_call | solution.py:269
  43.0 13.5 %all_to_all.16 = f32[32,1,2,640]{3,2,1,0:T(2,128)S(1)} all-to-all(f32[32,1,2,640]{3,2,1,0:T(2,128)S(1)} %broadcast_in_dim.11), channel_id=1, replica_groups={{20,0,1,2,3,4,5,6,7,8,9,10,11,12,13,14,15,16,17,18,19,21,22,23,24,25,26..., dimensions={0} | all-to-all | bytes 327680 | tf_op jit(solution)/shard_map/all_to_all | solution.py:197
  56.5 0.0 copy-done
  56.5 0.0 copy-done.3
  56.5 0.0 copy-done.4
  56.5 2.1 %shard_map.104 = bf16[4,4,64,1024]{3,2,1,0:T(8,128)(2,1)} custom-call(f32[4,256,1024]{2,1,0:T(8,128)S(1)} %get-tuple-element.34.refs_0_, bf16[4,4,64,1024]{3,2,1,0:T(8,128)(2,1)S(1)} %copy-done, f32[32,2,640]{2,1,0:T(2,128)S(1)} %bitcast.14, f32[1,1024]{1,0:T(1,128)S(1)} %bitcast.18, f32[1,1024]{1,0:T(1,128)S(1)} %bitcast.19, bf16[256,1024]{1,0:T(8,128)(2,1)S(1)} %copy-done.1), custom_call_target="tpu_custom_call" | custom-call | flops 8388608 | bytes 1048576 | tf_op jit(solution)/shard_map/pallas_call | solution.py:279
  (2 shorter events, 0.1 us)
Async XLA Ops:
  0.0 24.0 %copy-start.2 = (bf16[3,3,256,256]{3,2,1,0:T(8,128)(2,1)S(1)}, bf16[3,3,256,256]{3,2,1,0:T(8,128)(2,1)}, u32[]{:S(2)}) copy-start(bf16[3,3,256,256]{3,2,1,0:T(8,128)(2,1)} %param.12) | copy-start | bytes 3538948
  0.0 24.0 %copy-start.8 = (f32[256]{0:T(256)S(1)}, f32[256]{0:T(256)}, u32[]{:S(2)}) copy-start(f32[256]{0:T(256)} %param.15) | copy-start | bytes 3076
  0.0 24.0 %copy-start.7 = (f32[256]{0:T(256)S(1)}, f32[256]{0:T(256)}, u32[]{:S(2)}) copy-start(f32[256]{0:T(256)} %param.14) | copy-start | bytes 3076
  3.3 20.7 %all-to-all-start = ((f32[32,1,2,256]{3,2,1,0:T(2,128)}), f32[32,1,2,256]{3,2,1,0:T(2,128)S(1)}, u32[]{:S(2)}, u32[]{:S(2)}) async-start(f32[32,1,2,256]{3,2,1,0:T(2,128)} %broadcast_in_dim.9), calls=%async_computation | async-start | bytes 131072 | tf_op jit(solution)/shard_map/all_to_all | solution.py:197
  16.5 8.7 %collective-permute-start = (bf16[256,256]{1,0:T(8,128)(2,1)S(1)}, bf16[256,256]{1,0:T(8,128)(2,1)S(1)}, u32[]{:S(2)}, u32[]{:S(2)}) collective-permute-start(bf16[256,256]{1,0:T(8,128)(2,1)S(1)} %get-tuple-element.26), channel_id=1, source_target_pairs={{0,1},{2,3},{4,5},{6,7},{8,9},{10,11},{12,13},{14,15},{16,17},{18,... | collective-permute-start | bytes 393224 | tf_op jit(solution)/shard_map/ppermute | solution.py:240
  19.0 7.2 %collective-permute-start.1 = (bf16[256,256]{1,0:T(8,128)(2,1)S(1)}, bf16[256,256]{1,0:T(8,128)(2,1)S(1)}, u32[]{:S(2)}, u32[]{:S(2)}) collective-permute-start(bf16[256,256]{1,0:T(8,128)(2,1)S(1)} %get-tuple-element.27), channel_id=1, source_target_pairs={{1,2},{3,4},{5,6},{7,8},{9,10},{11,12},{13,14},{15,16},{17,18},{19... | collective-permute-start | bytes 393224 | tf_op jit(solution)/shard_map/ppermute | solution.py:239
  25.2 17.0 %copy-start.1 = (bf16[256,1024]{1,0:T(8,128)(2,1)S(1)}, bf16[256,1024]{1,0:T(8,128)(2,1)}, u32[]{:S(2)}) copy-start(bf16[256,1024]{1,0:T(8,128)(2,1)} %refs_5_.1) | copy-start | bytes 1572868
  25.2 17.0 %copy-start.5 = (f32[256]{0:T(256)S(1)}, f32[256]{0:T(256)}, u32[]{:S(2)}) copy-start(f32[256]{0:T(256)} %param.16) | copy-start | bytes 3076
  25.2 16.9 %copy-start.6 = (f32[256]{0:T(256)S(1)}, f32[256]{0:T(256)}, u32[]{:S(2)}) copy-start(f32[256]{0:T(256)} %param.17) | copy-start | bytes 3076
  26.2 30.3 %copy-start = (bf16[4,4,64,1024]{3,2,1,0:T(8,128)(2,1)S(1)}, bf16[4,4,64,1024]{3,2,1,0:T(8,128)(2,1)}, u32[]{:S(2)}) copy-start(bf16[4,4,64,1024]{3,2,1,0:T(8,128)(2,1)} %refs_1_) | copy-start | bytes 6291460
  26.2 30.3 %copy-start.3 = (f32[1024]{0:T(1024)S(1)}, f32[1024]{0:T(1024)}, u32[]{:S(2)}) copy-start(f32[1024]{0:T(1024)} %param.18) | copy-start | bytes 12292
  26.2 30.3 %copy-start.4 = (f32[1024]{0:T(1024)S(1)}, f32[1024]{0:T(1024)}, u32[]{:S(2)}) copy-start(f32[1024]{0:T(1024)} %param.19) | copy-start | bytes 12292
